TPU v7x, 32 devices: a whole 2x2x4 slice. The times are simulated.
32 devices in a mesh: tp: 4 (over z), cp: 2 (over x), dp: 4 (over y, core).
Axes of the slice: x: 2, y: 2, z: 4, core: 2. Of those that a mesh axis runs over, the one named last changes fastest.
Arguments:
- tokens: bfloat16 [2048, 7168], P(('dp', 'tp', 'cp')), parts along dimension 0, may hold values from -6 to 6
- router: bfloat16 [7168, 4], replicated, may hold values from -0.0625 to 0.0625
- gate_weight: bfloat16 [4, 7168, 1024], P('cp', None, 'tp'), may hold values from -0.0625 to 0.0625
- up_weight: bfloat16 [4, 7168, 1024], P('cp', None, 'tp'), may hold values from -0.0625 to 0.0625
- down_weight: bfloat16 [4, 1024, 7168], P('cp', 'tp'), may hold values from -0.1875 to 0.1875
- expert_ids: int32 [2048, 2], P(('dp', 'tp', 'cp')), parts along dimension 0, may hold values from 0 to 3, as said below
- slot_index: int32 [2048, 2], P(('dp', 'tp', 'cp')), parts along dimension 0, may hold values from -1 to 1, as said below
Outputs:
- moe_out: bfloat16 [2048, 7168], P(('dp', 'tp', 'cp')), parts along dimension 0
There are 4 independent parts, one for each index of `dp`. A program takes and returns all parts, laid end to end along the dimension named above; an argument that names none is the same for every part. Nothing has to cross between parts.
Inputs may be any that keep to these rules, and one draw needn't show every extreme that they name: `expert_ids`: each row names 2 different experts in rising order; in every part one expert is named by 32 or more rows of every block. slot_index[t, k] is the number of earlier copies to expert expert_ids[t, k] within token t's block (rows in order, then k in order) when that is below 2, else -1.
All inputs are finite; a program needn't handle non-finite values.
Results may differ from a plain program's by a relative error of at most 0.012.
Values may be sent and summed in bfloat16 or wider, within the bound.
A program may use at most 64 MiB of HBM per device.

v0:
```python
import functools

import jax
import jax.numpy as jnp
from jax import lax
from jax.experimental import pallas as pl
from jax.experimental.pallas import tpu as pltpu
from jax.sharding import PartitionSpec as P

CAP_DEV = 2
ROUTE_SCALE = 2.5
CHUNKS = 1
MESH = pl.DeviceIdType.MESH
NT = (((1,), (1,)), ((), ()))


def rows_of(pieces):
    return jnp.concatenate([p.astype(jnp.float32) for p in pieces], axis=0).astype(jnp.bfloat16)


def flip(index, bits):
    for b in range(bits.bit_length()):
        if (bits >> b) & 1:
            index = index + (1 - 2 * lax.rem(index // (1 << b), 2)) * (1 << b)
    return index


def exchange_kernel(
    n_tp, n_cp, nc,
    tok_hbm, rt_hbm, ids_hbm, slot_hbm, wg_hbm, wu_hbm, wd_hbm,
    pr, mix_hbm,
    ids_ref, slot_ref, tok, rt, wg, wu, wd, xs, xr, ps, mix_ref,
    in_sem, wsem, own_sem, s1, r1, s2, r2,
):
    n = n_tp * n_cp
    my_z, my_x = lax.axis_index("tp"), lax.axis_index("cp")
    me = my_z * n_cp + my_x
    local, width, ff = wg.shape
    dc = width // nc
    slots = n_cp * local * CAP_DEV
    pow2 = n & (n - 1) == 0
    order = list(range(n - 1, 0, -1))

    def peer(j):
        return flip(me, j) if pow2 else lax.rem(me + j, n)

    def source(j):
        return flip(me, j) if pow2 else lax.rem(me + n - j, n)

    def device(other):
        return {"tp": other // n_cp, "cp": lax.rem(other, n_cp)}

    index_copies = [
        pltpu.make_async_copy(ids_hbm, ids_ref, in_sem.at[nc + 2]),
        pltpu.make_async_copy(slot_hbm, slot_ref, in_sem.at[nc + 3]),
    ]
    for copy in index_copies:
        copy.start()
    tok_copies = []
    for c in range(nc):
        cols = pl.ds(c * dc, dc)
        copy = pltpu.make_async_copy(tok_hbm.at[:, cols], tok.at[:, cols], in_sem.at[c])
        copy.start()
        tok_copies.append(copy)
    rt_copy = pltpu.make_async_copy(rt_hbm, rt, in_sem.at[nc])
    rt_copy.start()

    barrier = pltpu.get_barrier_semaphore()
    for j in order:
        pl.semaphore_signal(barrier, inc=1, device_id=device(peer(j)), device_id_type=MESH)

    up_copies, down_copies = {}, {}
    for e in range(local):
        for c in range(nc):
            cols = pl.ds(c * dc, dc)
            pair = [
                pltpu.make_async_copy(wg_hbm.at[e, cols, :], wg.at[e, cols, :], wsem.at[0, e, c]),
                pltpu.make_async_copy(wu_hbm.at[e, cols, :], wu.at[e, cols, :], wsem.at[1, e, c]),
            ]
            for copy in pair:
                copy.start()
            up_copies[e, c] = pair
        for c in range(nc):
            cols = pl.ds(c * dc, dc)
            copy = pltpu.make_async_copy(wd_hbm.at[e, :, cols], wd.at[e, :, cols], wsem.at[2, e, c])
            copy.start()
            down_copies[e, c] = copy

    for copy in index_copies:
        copy.wait()
    ids0, ids1 = ids_ref[0:1, :], ids_ref[1:2, :]
    slot0, slot1 = slot_ref[0:1, :], slot_ref[1:2, :]
    target0 = jnp.where(slot0 >= 0, ids0 * CAP_DEV + slot0, -1)
    target1 = jnp.where(slot1 >= 0, ids1 * CAP_DEV + slot1, -1)
    row = lax.broadcasted_iota(jnp.int32, (slots, ids0.shape[1]), 0)
    placing = jnp.where((row == target0) | (row == target1), 1.0, 0.0).astype(jnp.bfloat16)

    sends = []

    def dispatch(e, c):
        for j in order:
            other = peer(j)
            copy = pltpu.make_async_remote_copy(
                src_ref=xs.at[e, c, lax.rem(other, n_cp)],
                dst_ref=xr.at[e, c, me],
                send_sem=s1.at[e, c, j],
                recv_sem=r1.at[e, c, j],
                device_id=device(other),
                device_id_type=MESH,
            )
            copy.start()
            sends.append(copy)
        xr[e, c, me] = xs[e, c, my_x]

    for c in range(nc):
        tok_copies[c].wait()
        cols = pl.ds(c * dc, dc)
        outgoing = jnp.dot(placing, tok[:, cols], preferred_element_type=jnp.float32)
        for x in range(n_cp):
            for e in range(local):
                at = (x * local + e) * CAP_DEV
                xs[e, c, x] = outgoing[at:at + CAP_DEV].astype(jnp.bfloat16)
        if c == 0:
            pl.semaphore_wait(barrier, n - 1)
        dispatch(0, c)
    for e in range(1, local):
        for c in range(nc):
            dispatch(e, c)

    rt_copy.wait()
    logits = lax.dot_general(rt[...], tok[...], NT, preferred_element_type=jnp.float32)
    affinity = 1.0 / (1.0 + jnp.exp(-logits))
    erow = lax.broadcasted_iota(jnp.int32, logits.shape, 0)
    chosen0 = jnp.sum(jnp.where(erow == ids0, affinity, 0.0), axis=0, keepdims=True)
    chosen1 = jnp.sum(jnp.where(erow == ids1, affinity, 0.0), axis=0, keepdims=True)
    total = chosen0 + chosen1
    share0 = ROUTE_SCALE * chosen0 / total
    share1 = ROUTE_SCALE * chosen1 / total
    wide = lax.broadcasted_iota(jnp.int32, (local * n * CAP_DEV, ids0.shape[1]), 0)
    which = lax.rem(wide // CAP_DEV, n_cp) * local + wide // (n * CAP_DEV)
    wide = which * CAP_DEV + lax.rem(wide, CAP_DEV)
    mix = jnp.where(wide == target0, share0, 0.0) + jnp.where(wide == target1, share1, 0.0)
    mix = mix.T
    mix_hi = mix.astype(jnp.bfloat16)
    mix_lo = (mix - mix_hi.astype(jnp.float32)).astype(jnp.bfloat16)
    mix_ref[...] = jnp.concatenate([mix_hi, mix_lo], axis=0)
    mix_copy = pltpu.make_async_copy(mix_ref, mix_hbm, in_sem.at[nc + 1])
    mix_copy.start()

    def arrival(ref, j, sem):
        pltpu.make_async_remote_copy(
            src_ref=ref, dst_ref=ref, send_sem=sem, recv_sem=sem,
            device_id=device(peer(j)), device_id_type=MESH,
        ).wait_recv()

    owns = []
    for e in range(local):
        gate = jnp.zeros((n * CAP_DEV, ff), jnp.float32)
        up = jnp.zeros((n * CAP_DEV, ff), jnp.float32)
        for c in range(nc):
            cols = pl.ds(c * dc, dc)
            for copy in up_copies[e, c]:
                copy.wait()
            for j in order:
                arrival(xr.at[e, c, source(j)], j, r1.at[e, c, j])
            x = rows_of([xr[e, c, i] for i in range(n)])
            gate += jnp.dot(x, wg[e, cols, :], preferred_element_type=jnp.float32)
            up += jnp.dot(x, wu[e, cols, :], preferred_element_type=jnp.float32)
        hidden = (gate / (1.0 + jnp.exp(-gate)) * up).astype(jnp.bfloat16)
        for c in range(nc):
            cols = pl.ds(c * dc, dc)
            down_copies[e, c].wait()
            part = jnp.dot(hidden, wd[e, :, cols], preferred_element_type=jnp.float32)
            for i in range(n):
                ps[e, c, i] = part[i * CAP_DEV:(i + 1) * CAP_DEV].astype(jnp.bfloat16)
            for j in order:
                other = peer(j)
                copy = pltpu.make_async_remote_copy(
                    src_ref=ps.at[e, c, other],
                    dst_ref=pr.at[e, c, me],
                    send_sem=s2.at[e, c, j],
                    recv_sem=r2.at[e, c, j],
                    device_id=device(other),
                    device_id_type=MESH,
                )
                copy.start()
                sends.append(copy)
            own = pltpu.make_async_copy(ps.at[e, c, me], pr.at[e, c, me], own_sem.at[e, c])
            own.start()
            owns.append(own)
    mix_copy.wait()
    for copy in owns:
        copy.wait()
    for copy in sends:
        copy.wait_send()
    for e in range(local):
        for c in range(nc):
            for j in order:
                arrival(pr.at[e, c, source(j)], j, r2.at[e, c, j])


def combine_kernel(pr_hbm, mix_hbm, out_hbm, pr, mix_ref, ob, isem, osem):
    local, nc, n, cap, dc = pr.shape
    mix_copy = pltpu.make_async_copy(mix_hbm, mix_ref, isem.at[nc])
    mix_copy.start()
    loads, outs = [], []
    for c in range(nc):
        copy = pltpu.make_async_copy(pr_hbm.at[:, c], pr.at[:, c], isem.at[c])
        copy.start()
        loads.append(copy)
    mix_copy.wait()
    mix = mix_ref[...]
    half = mix.shape[0] // 2
    for c in range(nc):
        loads[c].wait()
        rows = rows_of([pr[e, c, i] for e in range(local) for i in range(n)])
        for p in range(2):
            part = dc // 2
            cols = pl.ds(c * dc + p * part, part)
            both = jnp.dot(
                mix, rows[:, p * part:(p + 1) * part], preferred_element_type=jnp.float32
            )
            ob[:, cols] = (both[:half] + both[half:]).astype(jnp.bfloat16)
            copy = pltpu.make_async_copy(ob.at[:, cols], out_hbm.at[:, cols], osem.at[c, p])
            copy.start()
            outs.append(copy)
    for copy in outs:
        copy.wait()


def body(n_tp, n_cp, tokens, router, gate_weight, up_weight, down_weight, expert_ids, slot_index):
    n = n_tp * n_cp
    rows, width = tokens.shape
    local, _, ff = gate_weight.shape
    nc = CHUNKS if n <= 16 else 1
    dc = width // nc
    anywhere = pl.BlockSpec(memory_space=pl.ANY)
    bf16 = jnp.bfloat16
    dma = pltpu.SemaphoreType.DMA
    slab = (local, nc, n, CAP_DEV, dc)
    pr, mix = pl.pallas_call(
        functools.partial(exchange_kernel, n_tp, n_cp, nc),
        out_shape=[
            jax.ShapeDtypeStruct(slab, bf16),
            jax.ShapeDtypeStruct((2 * rows, local * n * CAP_DEV), bf16),
        ],
        in_specs=[anywhere] * 7,
        out_specs=[anywhere, anywhere],
        scratch_shapes=[
            pltpu.VMEM((expert_ids.shape[1], rows), jnp.int32),
            pltpu.VMEM((slot_index.shape[1], rows), jnp.int32),
            pltpu.VMEM((rows, width), bf16),
            pltpu.VMEM((router.shape[1], width), bf16),
            pltpu.VMEM((local, width, ff), bf16),
            pltpu.VMEM((local, width, ff), bf16),
            pltpu.VMEM((local, ff, width), bf16),
            pltpu.VMEM((local, nc, n_cp, CAP_DEV, dc), bf16),
            pltpu.VMEM(slab, bf16),
            pltpu.VMEM(slab, bf16),
            pltpu.VMEM((2 * rows, local * n * CAP_DEV), bf16),
            dma((nc + 4,)),
            dma((3, local, nc)),
            dma((local, nc)),
            dma((local, nc, n)),
            dma((local, nc, n)),
            dma((local, nc, n)),
            dma((local, nc, n)),
        ],
        compiler_params=pltpu.CompilerParams(
            collective_id=0, has_side_effects=True, vmem_limit_bytes=60 * 1024 * 1024
        ),
    )(tokens, router.T, expert_ids.T, slot_index.T, gate_weight, up_weight, down_weight)
    return pl.pallas_call(
        combine_kernel,
        out_shape=jax.ShapeDtypeStruct((rows, width), bf16),
        in_specs=[anywhere, anywhere],
        out_specs=anywhere,
        scratch_shapes=[
            pltpu.VMEM(slab, bf16),
            pltpu.VMEM(mix.shape, bf16),
            pltpu.VMEM((rows, width), bf16),
            dma((nc + 1,)),
            dma((nc, 2)),
        ],
    )(pr, mix)


def solution(mesh):
    in_specs = (
        P(("dp", "tp", "cp"), None),
        P(),
        P("cp", None, "tp"),
        P("cp", None, "tp"),
        P("cp", "tp", None),
        P(("dp", "tp", "cp"), None),
        P(("dp", "tp", "cp"), None),
    )
    out_specs = P(("dp", "tp", "cp"), None)
    step = functools.partial(body, mesh.shape["tp"], mesh.shape["cp"])
    return jax.shard_map(step, mesh=mesh, in_specs=in_specs, out_specs=out_specs, check_vma=False)
```

profile of v0, /device:TPU:0, one launch (start us, length us, event | category | flops | bytes accessed | tf_op | source)
XLA Modules:
  0.0 29.9 jit_solution(10503813464888287399)
XLA Ops:
  0.0 27.4 %shard_map.73 = (bf16[2,1,8,2,7168]{4,3,2,1,0:T(2,128)(2,1)}, bf16[128,32]{1,0:T(8,128)(2,1)}) custom-call(bf16[64,7168]{1,0:T(8,128)(2,1)} %tok_hbm.1, bf16[4,7168]{1,0:T(4,128)(2,1)} %bitcast.3, s32[2,64]{1,0:T(2,128)} %bitcast.4, s32[2,64]{1,0:T(2,128)} %bitcast.5, bf16[2,7168,256]{2,1,0:T(8,128)(2,1)} %wg_hbm.1, bf16[2,7168,256]{2,1,0:T(8,128)(2,1)} %wu_hbm.1, ...), custom_call_target="tpu_custom_call" | custom-call | tf_op jit(solution)/shard_map/pallas_call | solution.py:241
  27.4 2.5 %shard_map.74 = bf16[64,7168]{1,0:T(8,128)(2,1)} custom-call(bf16[2,1,8,2,7168]{4,3,2,1,0:T(2,128)(2,1)} %get-tuple-element.7.pr_hbm, bf16[128,32]{1,0:T(8,128)(2,1)} %get-tuple-element.8.mix_hbm), custom_call_target="tpu_custom_call" | custom-call | tf_op jit(solution)/shard_map/pallas_call | solution.py:273
where the time goes:
time: 30.1 us; the launch traced here: 29.9 us
  Pallas kernels  29.9 us (99%)
    pallas_call x1, Pallas kernels, body(): pl.pallas_call(functools.partial(exchange_kernel, n_tp, n_cp, nc), out_sh...  27.4 us
    pallas_call x1, Pallas kernels, body(): pl.pallas_call(combine_kernel, out_shape=jax.ShapeDtypeStruct((rows, widt...  2.49 us

commit v1 on v0

--- a/solution.py
+++ b/solution.py
@@ -10,6 +10,7 @@
 CAP_DEV = 2
 ROUTE_SCALE = 2.5
 CHUNKS = 1
+SPLIT = 4
 MESH = pl.DeviceIdType.MESH
 NT = (((1,), (1,)), ((), ()))
 
@@ -28,9 +29,9 @@
 def exchange_kernel(
     n_tp, n_cp, nc,
     tok_hbm, rt_hbm, ids_hbm, slot_hbm, wg_hbm, wu_hbm, wd_hbm,
-    pr, mix_hbm,
-    ids_ref, slot_ref, tok, rt, wg, wu, wd, xs, xr, ps, mix_ref,
-    in_sem, wsem, own_sem, s1, r1, s2, r2,
+    pr, mix_ref,
+    ids_ref, slot_ref, tok, rt, wg, wu, wd, xs, xr, ps,
+    in_sem, wsem, s1, r1, s2, r2,
 ):
     n = n_tp * n_cp
     my_z, my_x = lax.axis_index("tp"), lax.axis_index("cp")
@@ -51,8 +52,8 @@
         return {"tp": other // n_cp, "cp": lax.rem(other, n_cp)}
 
     index_copies = [
-        pltpu.make_async_copy(ids_hbm, ids_ref, in_sem.at[nc + 2]),
-        pltpu.make_async_copy(slot_hbm, slot_ref, in_sem.at[nc + 3]),
+        pltpu.make_async_copy(ids_hbm, ids_ref, in_sem.at[nc + 1]),
+        pltpu.make_async_copy(slot_hbm, slot_ref, in_sem.at[nc + 2]),
     ]
     for copy in index_copies:
         copy.start()
@@ -95,21 +96,17 @@
     row = lax.broadcasted_iota(jnp.int32, (slots, ids0.shape[1]), 0)
     placing = jnp.where((row == target0) | (row == target1), 1.0, 0.0).astype(jnp.bfloat16)
 
-    sends = []
-
     def dispatch(e, c):
         for j in order:
             other = peer(j)
-            copy = pltpu.make_async_remote_copy(
+            pltpu.make_async_remote_copy(
                 src_ref=xs.at[e, c, lax.rem(other, n_cp)],
                 dst_ref=xr.at[e, c, me],
-                send_sem=s1.at[e, c, j],
-                recv_sem=r1.at[e, c, j],
+                send_sem=s1,
+                recv_sem=r1.at[e, c],
                 device_id=device(other),
                 device_id_type=MESH,
-            )
-            copy.start()
-            sends.append(copy)
+            ).start()
         xr[e, c, me] = xs[e, c, my_x]
 
     for c in range(nc):
@@ -144,16 +141,10 @@
     mix_hi = mix.astype(jnp.bfloat16)
     mix_lo = (mix - mix_hi.astype(jnp.float32)).astype(jnp.bfloat16)
     mix_ref[...] = jnp.concatenate([mix_hi, mix_lo], axis=0)
-    mix_copy = pltpu.make_async_copy(mix_ref, mix_hbm, in_sem.at[nc + 1])
-    mix_copy.start()
-
-    def arrival(ref, j, sem):
-        pltpu.make_async_remote_copy(
-            src_ref=ref, dst_ref=ref, send_sem=sem, recv_sem=sem,
-            device_id=device(peer(j)), device_id_type=MESH,
-        ).wait_recv()
-
-    owns = []
+
+    def drain(ref, sem):
+        pltpu.make_async_copy(ref, ref, sem).wait()
+
     for e in range(local):
         gate = jnp.zeros((n * CAP_DEV, ff), jnp.float32)
         up = jnp.zeros((n * CAP_DEV, ff), jnp.float32)
@@ -161,8 +152,7 @@
             cols = pl.ds(c * dc, dc)
             for copy in up_copies[e, c]:
                 copy.wait()
-            for j in order:
-                arrival(xr.at[e, c, source(j)], j, r1.at[e, c, j])
+            drain(xr.at[e, c, pl.ds(0, n - 1)], r1.at[e, c])
             x = rows_of([xr[e, c, i] for i in range(n)])
             gate += jnp.dot(x, wg[e, cols, :], preferred_element_type=jnp.float32)
             up += jnp.dot(x, wu[e, cols, :], preferred_element_type=jnp.float32)
@@ -173,53 +163,35 @@
             part = jnp.dot(hidden, wd[e, :, cols], preferred_element_type=jnp.float32)
             for i in range(n):
                 ps[e, c, i] = part[i * CAP_DEV:(i + 1) * CAP_DEV].astype(jnp.bfloat16)
-            for j in order:
-                other = peer(j)
-                copy = pltpu.make_async_remote_copy(
-                    src_ref=ps.at[e, c, other],
-                    dst_ref=pr.at[e, c, me],
-                    send_sem=s2.at[e, c, j],
-                    recv_sem=r2.at[e, c, j],
-                    device_id=device(other),
-                    device_id_type=MESH,
-                )
-                copy.start()
-                sends.append(copy)
-            own = pltpu.make_async_copy(ps.at[e, c, me], pr.at[e, c, me], own_sem.at[e, c])
-            own.start()
-            owns.append(own)
-    mix_copy.wait()
-    for copy in owns:
-        copy.wait()
-    for copy in sends:
-        copy.wait_send()
-    for e in range(local):
-        for c in range(nc):
-            for j in order:
-                arrival(pr.at[e, c, source(j)], j, r2.at[e, c, j])
-
-
-def combine_kernel(pr_hbm, mix_hbm, out_hbm, pr, mix_ref, ob, isem, osem):
+            for other in range(n):
+                @pl.when(other != me)
+                def _():
+                    pltpu.make_async_remote_copy(
+                        src_ref=ps.at[e, c, other],
+                        dst_ref=pr.at[e, c, me],
+                        send_sem=s2,
+                        recv_sem=r2,
+                        device_id=device(jnp.int32(other)),
+                        device_id_type=MESH,
+                    ).start()
+            pr[e, c, me] = ps[e, c, me]
+    drain(xr.at[:, :, pl.ds(0, n - 1)], s1)
+    drain(pr.at[:, :, pl.ds(0, n - 1)], s2)
+    drain(pr.at[:, :, pl.ds(0, n - 1)], r2)
+
+
+def combine_kernel(pr, mix_ref, out_hbm, ob, osem):
     local, nc, n, cap, dc = pr.shape
-    mix_copy = pltpu.make_async_copy(mix_hbm, mix_ref, isem.at[nc])
-    mix_copy.start()
-    loads, outs = [], []
-    for c in range(nc):
-        copy = pltpu.make_async_copy(pr_hbm.at[:, c], pr.at[:, c], isem.at[c])
-        copy.start()
-        loads.append(copy)
-    mix_copy.wait()
     mix = mix_ref[...]
     half = mix.shape[0] // 2
+    part = dc // SPLIT
+    outs = []
     for c in range(nc):
-        loads[c].wait()
-        rows = rows_of([pr[e, c, i] for e in range(local) for i in range(n)])
-        for p in range(2):
-            part = dc // 2
+        for p in range(SPLIT):
+            at = pl.ds(p * part, part)
             cols = pl.ds(c * dc + p * part, part)
-            both = jnp.dot(
-                mix, rows[:, p * part:(p + 1) * part], preferred_element_type=jnp.float32
-            )
+            rows = rows_of([pr[e, c, i, :, at] for e in range(local) for i in range(n)])
+            both = jnp.dot(mix, rows, preferred_element_type=jnp.float32)
             ob[:, cols] = (both[:half] + both[half:]).astype(jnp.bfloat16)
             copy = pltpu.make_async_copy(ob.at[:, cols], out_hbm.at[:, cols], osem.at[c, p])
             copy.start()
@@ -235,17 +207,18 @@
     nc = CHUNKS if n <= 16 else 1
     dc = width // nc
     anywhere = pl.BlockSpec(memory_space=pl.ANY)
+    resident = pl.BlockSpec(memory_space=pltpu.VMEM)
     bf16 = jnp.bfloat16
     dma = pltpu.SemaphoreType.DMA
     slab = (local, nc, n, CAP_DEV, dc)
     pr, mix = pl.pallas_call(
         functools.partial(exchange_kernel, n_tp, n_cp, nc),
         out_shape=[
-            jax.ShapeDtypeStruct(slab, bf16),
-            jax.ShapeDtypeStruct((2 * rows, local * n * CAP_DEV), bf16),
+            pltpu.VMEM(slab, bf16),
+            pltpu.VMEM((2 * rows, local * n * CAP_DEV), bf16),
         ],
         in_specs=[anywhere] * 7,
-        out_specs=[anywhere, anywhere],
+        out_specs=[resident, resident],
         scratch_shapes=[
             pltpu.VMEM((expert_ids.shape[1], rows), jnp.int32),
             pltpu.VMEM((slot_index.shape[1], rows), jnp.int32),
@@ -257,14 +230,12 @@
             pltpu.VMEM((local, nc, n_cp, CAP_DEV, dc), bf16),
             pltpu.VMEM(slab, bf16),
             pltpu.VMEM(slab, bf16),
-            pltpu.VMEM((2 * rows, local * n * CAP_DEV), bf16),
-            dma((nc + 4,)),
+            dma((nc + 3,)),
             dma((3, local, nc)),
+            dma,
             dma((local, nc)),
-            dma((local, nc, n)),
-            dma((local, nc, n)),
-            dma((local, nc, n)),
-            dma((local, nc, n)),
+            dma,
+            dma,
         ],
         compiler_params=pltpu.CompilerParams(
             collective_id=0, has_side_effects=True, vmem_limit_bytes=60 * 1024 * 1024
@@ -273,15 +244,13 @@
     return pl.pallas_call(
         combine_kernel,
         out_shape=jax.ShapeDtypeStruct((rows, width), bf16),
-        in_specs=[anywhere, anywhere],
+        in_specs=[resident, resident],
         out_specs=anywhere,
         scratch_shapes=[
-            pltpu.VMEM(slab, bf16),
-            pltpu.VMEM(mix.shape, bf16),
             pltpu.VMEM((rows, width), bf16),
-            dma((nc + 1,)),
-            dma((nc, 2)),
+            dma((nc, SPLIT)),
         ],
+        compiler_params=pltpu.CompilerParams(vmem_limit_bytes=8 * 1024 * 1024),
     )(pr, mix)
 
 

time: 30.1 us -> 26.8 us (0.89)
  Pallas kernels: 29.9 us -> 26.6 us
    pallas_call x1, Pallas kernels: 27.4 us -> 25.3 us  [body(): pl.pallas_call(functools.partial(exchange_kernel, n_tp, n_cp, nc), out_sh...]
    pallas_call x1, Pallas kernels: 2.49 us -> 1.37 us  [body(): pl.pallas_call(combine_kernel, out_shape=jax.ShapeDtypeStruct((rows, widt...]
where the time goes in v1:
time: 26.8 us; the launch traced here: 26.7 us
  Pallas kernels  26.6 us (99%)
    pallas_call x1, Pallas kernels, body(): pl.pallas_call(functools.partial(exchange_kernel, n_tp, n_cp, nc), out_sh...  25.3 us
    pallas_call x1, Pallas kernels, body(): pl.pallas_call(combine_kernel, out_shape=jax.ShapeDtypeStruct((rows, widt...  1.37 us

profile of v1, /device:TPU:0, one launch (start us, length us, event | category | flops | bytes accessed | tf_op | source)
XLA Modules:
  0.0 26.7 jit_solution(5523954380826743164)
XLA Ops:
  0.0 25.3 %shard_map.73 = (bf16[2,1,8,2,7168]{4,3,2,1,0:T(2,128)(2,1)S(1)}, bf16[128,32]{1,0:T(8,128)(2,1)S(1)}) custom-call(bf16[64,7168]{1,0:T(8,128)(2,1)} %tok_hbm.1, bf16[4,7168]{1,0:T(4,128)(2,1)} %bitcast.3, s32[2,64]{1,0:T(2,128)} %bitcast.4, s32[2,64]{1,0:T(2,128)} %bitcast.5, bf16[2,7168,256]{2,1,0:T(8,128)(2,1)} %wg_hbm.1, bf16[2,7168,256]{2,1,0:T(8,128)(2,1)} %wu_hbm.1, ...), custom_call_target="tpu_custom_call" | custom-call | tf_op jit(solution)/shard_map/pallas_call | solution.py:214
  25.3 1.4 %shard_map.74 = bf16[64,7168]{1,0:T(8,128)(2,1)} custom-call(bf16[2,1,8,2,7168]{4,3,2,1,0:T(2,128)(2,1)S(1)} %get-tuple-element.7.pr, bf16[128,32]{1,0:T(8,128)(2,1)S(1)} %get-tuple-element.8.mix_ref), custom_call_target="tpu_custom_call" | custom-call | tf_op jit(solution)/shard_map/pallas_call | solution.py:244

commit v2 on v1

--- a/solution.py
+++ b/solution.py
@@ -31,7 +31,7 @@
     tok_hbm, rt_hbm, ids_hbm, slot_hbm, wg_hbm, wu_hbm, wd_hbm,
     pr, mix_ref,
     ids_ref, slot_ref, tok, rt, wg, wu, wd, xs, xr, ps,
-    in_sem, wsem, s1, r1, s2, r2,
+    in_sem, wsem, s1, r1, fs, fr, s2, r2,
 ):
     n = n_tp * n_cp
     my_z, my_x = lax.axis_index("tp"), lax.axis_index("cp")
@@ -40,6 +40,8 @@
     dc = width // nc
     slots = n_cp * local * CAP_DEV
     pow2 = n & (n - 1) == 0
+    h = n_tp // 2 if n_tp % 2 == 0 and n_tp > 2 else n_tp
+    inner = (h - 1, h)
     order = list(range(n - 1, 0, -1))
 
     def peer(j):
@@ -50,6 +52,9 @@
 
     def device(other):
         return {"tp": other // n_cp, "cp": lax.rem(other, n_cp)}
+
+    def drain(ref, sem):
+        pltpu.make_async_copy(ref, ref, sem).wait()
 
     index_copies = [
         pltpu.make_async_copy(ids_hbm, ids_ref, in_sem.at[nc + 1]),
@@ -96,18 +101,71 @@
     row = lax.broadcasted_iota(jnp.int32, (slots, ids0.shape[1]), 0)
     placing = jnp.where((row == target0) | (row == target1), 1.0, 0.0).astype(jnp.bfloat16)
 
+    half = my_z // h
+    gateway = (my_z == inner[0]) | (my_z == inner[-1])
+    pair = range(n_tp // h)
+
+    def place(e, c, z, x, recv_sem):
+        pltpu.make_async_remote_copy(
+            src_ref=xs.at[e, c, x],
+            dst_ref=xr.at[e, c, me],
+            send_sem=s1,
+            recv_sem=recv_sem,
+            device_id={"tp": jnp.int32(z), "cp": jnp.int32(x)},
+            device_id_type=MESH,
+        ).start()
+
     def dispatch(e, c):
-        for j in order:
-            other = peer(j)
-            pltpu.make_async_remote_copy(
-                src_ref=xs.at[e, c, lax.rem(other, n_cp)],
-                dst_ref=xr.at[e, c, me],
-                send_sem=s1,
-                recv_sem=r1.at[e, c],
-                device_id=device(other),
-                device_id_type=MESH,
-            ).start()
+        for b in pair:
+            for z in [inner[b]] + [z for z in range(b * h, b * h + h) if z != inner[b]]:
+                if h == n_tp:
+                    continue
+                @pl.when((half != b) if z == inner[b] else (half != b) & gateway)
+                def _():
+                    for x in range(n_cp):
+                        place(e, c, z, x, fr.at[e, c, lax.rem(me, h * n_cp)])
+        for z in range(n_tp):
+            for x in range(n_cp):
+                @pl.when((half == z // h) & (me != z * n_cp + x))
+                def _():
+                    place(e, c, z, x, r1.at[e, c])
         xr[e, c, me] = xs[e, c, my_x]
+
+    def across(k):
+        return (1 - half) * (h * n_cp) + k
+
+    def forward(e, c):
+        for b in pair if h < n_tp else ():
+            @pl.when(my_z == inner[b])
+            def _():
+                far = [z for z in range((1 - b) * h, (1 - b) * h + h) if z != inner[1 - b]]
+                near = [z for z in range(b * h, b * h + h) if z != inner[b]]
+                for k in [z * n_cp + x for z in far for x in range(n_cp)]:
+                    drain(xr.at[e, c, k], fr.at[e, c, k % (h * n_cp)])
+                    for m, z in enumerate(near):
+                        pltpu.make_async_remote_copy(
+                            src_ref=xr.at[e, c, k],
+                            dst_ref=xr.at[e, c, k],
+                            send_sem=fs.at[m],
+                            recv_sem=fr.at[e, c, k % (h * n_cp)],
+                            device_id={"tp": jnp.int32(z), "cp": my_x},
+                            device_id_type=MESH,
+                        ).start()
+
+    def collect(e, c):
+        if h * n_cp > 1:
+            drain(xr.at[e, c, pl.ds(0, h * n_cp - 1)], r1.at[e, c])
+        for b in pair if h < n_tp else ():
+            other = range((1 - b) * h, (1 - b) * h + h)
+            @pl.when(half == b)
+            def _():
+                for x in range(n_cp):
+                    k = inner[1 - b] * n_cp + x
+                    drain(xr.at[e, c, k], fr.at[e, c, k % (h * n_cp)])
+            @pl.when((half == b) & jnp.logical_not(gateway))
+            def _():
+                for k in [z * n_cp + x for z in other if z != inner[1 - b] for x in range(n_cp)]:
+                    drain(xr.at[e, c, k], fr.at[e, c, k % (h * n_cp)])
 
     for c in range(nc):
         tok_copies[c].wait()
@@ -142,9 +200,8 @@
     mix_lo = (mix - mix_hi.astype(jnp.float32)).astype(jnp.bfloat16)
     mix_ref[...] = jnp.concatenate([mix_hi, mix_lo], axis=0)
 
-    def drain(ref, sem):
-        pltpu.make_async_copy(ref, ref, sem).wait()
-
+    for c in range(nc):
+        forward(0, c)
     for e in range(local):
         gate = jnp.zeros((n * CAP_DEV, ff), jnp.float32)
         up = jnp.zeros((n * CAP_DEV, ff), jnp.float32)
@@ -152,10 +209,12 @@
             cols = pl.ds(c * dc, dc)
             for copy in up_copies[e, c]:
                 copy.wait()
-            drain(xr.at[e, c, pl.ds(0, n - 1)], r1.at[e, c])
+            collect(e, c)
             x = rows_of([xr[e, c, i] for i in range(n)])
             gate += jnp.dot(x, wg[e, cols, :], preferred_element_type=jnp.float32)
             up += jnp.dot(x, wu[e, cols, :], preferred_element_type=jnp.float32)
+        for c in range(nc if e + 1 < local else 0):
+            forward(e + 1, c)
         hidden = (gate / (1.0 + jnp.exp(-gate)) * up).astype(jnp.bfloat16)
         for c in range(nc):
             cols = pl.ds(c * dc, dc)
@@ -175,7 +234,17 @@
                         device_id_type=MESH,
                     ).start()
             pr[e, c, me] = ps[e, c, me]
-    drain(xr.at[:, :, pl.ds(0, n - 1)], s1)
+    if h < n_tp:
+        @pl.when(gateway)
+        def _():
+            drain(xr.at[:, :, pl.ds(0, 2 * h * n_cp - 1)], s1)
+            for m in range(h - 1):
+                drain(xr.at[:, :, pl.ds(0, (h - 1) * n_cp)], fs.at[m])
+        @pl.when(jnp.logical_not(gateway))
+        def _():
+            drain(xr.at[:, :, pl.ds(0, h * n_cp - 1 + n_cp)], s1)
+    else:
+        drain(xr.at[:, :, pl.ds(0, n - 1)], s1)
     drain(pr.at[:, :, pl.ds(0, n - 1)], s2)
     drain(pr.at[:, :, pl.ds(0, n - 1)], r2)
 
@@ -234,6 +303,8 @@
             dma((3, local, nc)),
             dma,
             dma((local, nc)),
+            dma((max(n_tp // 2 - 1, 1),)),
+            dma((local, nc, max(n_tp // 2, 1) * n_cp)),
             dma,
             dma,
         ],

time: 26.8 us -> 25.7 us (0.959)
  Pallas kernels: 26.6 us -> 25.5 us
    pallas_call x1, Pallas kernels: 25.3 us -> 24.2 us  [body(): pl.pallas_call(functools.partial(exchange_kernel, n_tp, n_cp, nc), out_sh...]
where the time goes in v2:
time: 25.7 us; the launch traced here: 25.6 us
  Pallas kernels  25.5 us (99%)
    pallas_call x1, Pallas kernels, body(): pl.pallas_call(functools.partial(exchange_kernel, n_tp, n_cp, nc), out_sh...  24.2 us
    pallas_call x1, Pallas kernels, body(): pl.pallas_call(combine_kernel, out_shape=jax.ShapeDtypeStruct((rows, widt...  1.36 us

profile of v2, /device:TPU:0, one launch (start us, length us, event | category | flops | bytes accessed | tf_op | source)
XLA Modules:
  0.0 25.6 jit_solution(10993112718587697223)
XLA Ops:
  0.0 24.2 %shard_map.73 = (bf16[2,1,8,2,7168]{4,3,2,1,0:T(2,128)(2,1)S(1)}, bf16[128,32]{1,0:T(8,128)(2,1)S(1)}) custom-call(bf16[64,7168]{1,0:T(8,128)(2,1)} %tok_hbm.1, bf16[4,7168]{1,0:T(4,128)(2,1)} %bitcast.3, s32[2,64]{1,0:T(2,128)} %bitcast.4, s32[2,64]{1,0:T(2,128)} %bitcast.5, bf16[2,7168,256]{2,1,0:T(8,128)(2,1)} %wg_hbm.1, bf16[2,7168,256]{2,1,0:T(8,128)(2,1)} %wu_hbm.1, ...), custom_call_target="tpu_custom_call" | custom-call | tf_op jit(solution)/shard_map/pallas_call | solution.py:283
  24.2 1.4 %shard_map.74 = bf16[64,7168]{1,0:T(8,128)(2,1)} custom-call(bf16[2,1,8,2,7168]{4,3,2,1,0:T(2,128)(2,1)S(1)} %get-tuple-element.7.pr, bf16[128,32]{1,0:T(8,128)(2,1)S(1)} %get-tuple-element.8.mix_ref), custom_call_target="tpu_custom_call" | custom-call | tf_op jit(solution)/shard_map/pallas_call | solution.py:315

commit v3 on v2

--- a/solution.py
+++ b/solution.py
@@ -11,6 +11,9 @@
 ROUTE_SCALE = 2.5
 CHUNKS = 1
 SPLIT = 4
+RELAY = (1, 1)
+SHARE_FIRST = False
+EARLY = True
 MESH = pl.DeviceIdType.MESH
 NT = (((1,), (1,)), ((), ()))
 
@@ -42,6 +45,7 @@
     pow2 = n & (n - 1) == 0
     h = n_tp // 2 if n_tp % 2 == 0 and n_tp > 2 else n_tp
     inner = (h - 1, h)
+    relay = [RELAY[min(e + 2 - local, 1)] if local > 1 else 1 for e in range(local)]
     order = list(range(n - 1, 0, -1))
 
     def peer(j):
@@ -104,26 +108,32 @@
     half = my_z // h
     gateway = (my_z == inner[0]) | (my_z == inner[-1])
     pair = range(n_tp // h)
+    near = [range(b * h, b * h + h) for b in pair]
 
     def place(e, c, z, x, recv_sem):
         pltpu.make_async_remote_copy(
             src_ref=xs.at[e, c, x],
             dst_ref=xr.at[e, c, me],
-            send_sem=s1,
+            send_sem=s1.at[e],
             recv_sem=recv_sem,
             device_id={"tp": jnp.int32(z), "cp": jnp.int32(x)},
             device_id_type=MESH,
         ).start()
 
-    def dispatch(e, c):
-        for b in pair:
-            for z in [inner[b]] + [z for z in range(b * h, b * h + h) if z != inner[b]]:
-                if h == n_tp:
+    def cross(e, c):
+        for b in pair if h < n_tp else ():
+            for z in sorted(near[b], key=lambda z: z != inner[b]):
+                ahead = half != b
+                if z != inner[b] and relay[e] == 2:
                     continue
-                @pl.when((half != b) if z == inner[b] else (half != b) & gateway)
+                if z != inner[b] and relay[e] == 1:
+                    ahead = ahead & gateway
+                @pl.when(ahead)
                 def _():
                     for x in range(n_cp):
                         place(e, c, z, x, fr.at[e, c, lax.rem(me, h * n_cp)])
+
+    def share(e, c):
         for z in range(n_tp):
             for x in range(n_cp):
                 @pl.when((half == z // h) & (me != z * n_cp + x))
@@ -131,22 +141,26 @@
                     place(e, c, z, x, r1.at[e, c])
         xr[e, c, me] = xs[e, c, my_x]
 
-    def across(k):
-        return (1 - half) * (h * n_cp) + k
-
-    def forward(e, c):
-        for b in pair if h < n_tp else ():
+    def sources(b, e, outer):
+        mine = inner[1 - b]
+        return [
+            z * n_cp + x
+            for z in near[1 - b] if (z != mine) == outer
+            for x in range(n_cp)
+        ]
+
+    def forward(e, c, outer):
+        for b in pair if h < n_tp and relay[e] > (0 if outer else 1) else ():
             @pl.when(my_z == inner[b])
             def _():
-                far = [z for z in range((1 - b) * h, (1 - b) * h + h) if z != inner[1 - b]]
-                near = [z for z in range(b * h, b * h + h) if z != inner[b]]
-                for k in [z * n_cp + x for z in far for x in range(n_cp)]:
+                others = [z for z in near[b] if z != inner[b]]
+                for k in sources(b, e, outer):
                     drain(xr.at[e, c, k], fr.at[e, c, k % (h * n_cp)])
-                    for m, z in enumerate(near):
+                    for m, z in enumerate(others):
                         pltpu.make_async_remote_copy(
                             src_ref=xr.at[e, c, k],
                             dst_ref=xr.at[e, c, k],
-                            send_sem=fs.at[m],
+                            send_sem=fs.at[e, m],
                             recv_sem=fr.at[e, c, k % (h * n_cp)],
                             device_id={"tp": jnp.int32(z), "cp": my_x},
                             device_id_type=MESH,
@@ -156,16 +170,14 @@
         if h * n_cp > 1:
             drain(xr.at[e, c, pl.ds(0, h * n_cp - 1)], r1.at[e, c])
         for b in pair if h < n_tp else ():
-            other = range((1 - b) * h, (1 - b) * h + h)
-            @pl.when(half == b)
-            def _():
-                for x in range(n_cp):
-                    k = inner[1 - b] * n_cp + x
-                    drain(xr.at[e, c, k], fr.at[e, c, k % (h * n_cp)])
-            @pl.when((half == b) & jnp.logical_not(gateway))
-            def _():
-                for k in [z * n_cp + x for z in other if z != inner[1 - b] for x in range(n_cp)]:
-                    drain(xr.at[e, c, k], fr.at[e, c, k % (h * n_cp)])
+            for outer in (False, True):
+                late = half == b
+                if relay[e] > (0 if outer else 1):
+                    late = late & jnp.logical_not(gateway)
+                @pl.when(late)
+                def _():
+                    for k in sources(b, e, outer):
+                        drain(xr.at[e, c, k], fr.at[e, c, k % (h * n_cp)])
 
     for c in range(nc):
         tok_copies[c].wait()
@@ -177,10 +189,19 @@
                 xs[e, c, x] = outgoing[at:at + CAP_DEV].astype(jnp.bfloat16)
         if c == 0:
             pl.semaphore_wait(barrier, n - 1)
-        dispatch(0, c)
+        cross(0, c)
+        if SHARE_FIRST:
+            share(0, c)
+    if not SHARE_FIRST:
+        for c in range(nc):
+            if local > 1:
+                cross(1, c)
+            share(0, c)
     for e in range(1, local):
         for c in range(nc):
-            dispatch(e, c)
+            if SHARE_FIRST or e > 1:
+                cross(e, c)
+            share(e, c)
 
     rt_copy.wait()
     logits = lax.dot_general(rt[...], tok[...], NT, preferred_element_type=jnp.float32)
@@ -200,8 +221,11 @@
     mix_lo = (mix - mix_hi.astype(jnp.float32)).astype(jnp.bfloat16)
     mix_ref[...] = jnp.concatenate([mix_hi, mix_lo], axis=0)
 
-    for c in range(nc):
-        forward(0, c)
+    for e in range(local):
+        for c in range(nc):
+            forward(e, c, False)
+            if e == 0 or EARLY:
+                forward(e, c, True)
     for e in range(local):
         gate = jnp.zeros((n * CAP_DEV, ff), jnp.float32)
         up = jnp.zeros((n * CAP_DEV, ff), jnp.float32)
@@ -213,8 +237,8 @@
             x = rows_of([xr[e, c, i] for i in range(n)])
             gate += jnp.dot(x, wg[e, cols, :], preferred_element_type=jnp.float32)
             up += jnp.dot(x, wu[e, cols, :], preferred_element_type=jnp.float32)
-        for c in range(nc if e + 1 < local else 0):
-            forward(e + 1, c)
+        for c in range(nc if e + 1 < local and not EARLY else 0):
+            forward(e + 1, c, True)
         hidden = (gate / (1.0 + jnp.exp(-gate)) * up).astype(jnp.bfloat16)
         for c in range(nc):
             cols = pl.ds(c * dc, dc)
@@ -234,17 +258,19 @@
                         device_id_type=MESH,
                     ).start()
             pr[e, c, me] = ps[e, c, me]
-    if h < n_tp:
+    for e in range(local):
+        own = h * n_cp - 1
+        if h == n_tp or relay[e] == 0:
+            drain(xr.at[e, :, pl.ds(0, n - 1)], s1.at[e])
+            continue
         @pl.when(gateway)
         def _():
-            drain(xr.at[:, :, pl.ds(0, 2 * h * n_cp - 1)], s1)
+            drain(xr.at[e, :, pl.ds(0, own + (h * n_cp if relay[e] == 1 else n_cp))], s1.at[e])
             for m in range(h - 1):
-                drain(xr.at[:, :, pl.ds(0, (h - 1) * n_cp)], fs.at[m])
+                drain(xr.at[e, :, pl.ds(0, (h - 2 + relay[e]) * n_cp)], fs.at[e, m])
         @pl.when(jnp.logical_not(gateway))
         def _():
-            drain(xr.at[:, :, pl.ds(0, h * n_cp - 1 + n_cp)], s1)
-    else:
-        drain(xr.at[:, :, pl.ds(0, n - 1)], s1)
+            drain(xr.at[e, :, pl.ds(0, own + n_cp)], s1.at[e])
     drain(pr.at[:, :, pl.ds(0, n - 1)], s2)
     drain(pr.at[:, :, pl.ds(0, n - 1)], r2)
 
@@ -301,9 +327,9 @@
             pltpu.VMEM(slab, bf16),
             dma((nc + 3,)),
             dma((3, local, nc)),
-            dma,
+            dma((local,)),
             dma((local, nc)),
-            dma((max(n_tp // 2 - 1, 1),)),
+            dma((local, max(n_tp // 2 - 1, 1))),
             dma((local, nc, max(n_tp // 2, 1) * n_cp)),
             dma,
             dma,

time: 25.7 us -> 25.1 us (0.977)
  Pallas kernels: 25.5 us -> 25 us
    pallas_call x1, Pallas kernels: 24.2 us -> 23.6 us  [body(): pl.pallas_call(functools.partial(exchange_kernel, n_tp, n_cp, nc), out_sh...]
where the time goes in v3:
time: 25.1 us; the launch traced here: 25 us
  Pallas kernels  25 us (100%)
    pallas_call x1, Pallas kernels, body(): pl.pallas_call(functools.partial(exchange_kernel, n_tp, n_cp, nc), out_sh...  23.6 us
    pallas_call x1, Pallas kernels, body(): pl.pallas_call(combine_kernel, out_shape=jax.ShapeDtypeStruct((rows, widt...  1.37 us

profile of v3, /device:TPU:0, one launch (start us, length us, event | category | flops | bytes accessed | tf_op | source)
XLA Modules:
  0.0 25.0 jit_solution(17668998412158780468)
XLA Ops:
  0.0 23.6 %shard_map.73 = (bf16[2,1,8,2,7168]{4,3,2,1,0:T(2,128)(2,1)S(1)}, bf16[128,32]{1,0:T(8,128)(2,1)S(1)}) custom-call(bf16[64,7168]{1,0:T(8,128)(2,1)} %tok_hbm.1, bf16[4,7168]{1,0:T(4,128)(2,1)} %bitcast.3, s32[2,64]{1,0:T(2,128)} %bitcast.4, s32[2,64]{1,0:T(2,128)} %bitcast.5, bf16[2,7168,256]{2,1,0:T(8,128)(2,1)} %wg_hbm.1, bf16[2,7168,256]{2,1,0:T(8,128)(2,1)} %wu_hbm.1, ...), custom_call_target="tpu_custom_call" | custom-call | tf_op jit(solution)/shard_map/pallas_call | solution.py:309
  23.6 1.4 %shard_map.74 = bf16[64,7168]{1,0:T(8,128)(2,1)} custom-call(bf16[2,1,8,2,7168]{4,3,2,1,0:T(2,128)(2,1)S(1)} %get-tuple-element.7.pr, bf16[128,32]{1,0:T(8,128)(2,1)S(1)} %get-tuple-element.8.mix_ref), custom_call_target="tpu_custom_call" | custom-call | tf_op jit(solution)/shard_map/pallas_call | solution.py:341

commit v4 on v3

--- a/solution.py
+++ b/solution.py
@@ -11,6 +11,7 @@
 ROUTE_SCALE = 2.5
 CHUNKS = 1
 SPLIT = 4
+MERGE = lambda z, h, e: 0 < z < h and e == 0
 RELAY = (1, 1)
 SHARE_FIRST = False
 EARLY = True
@@ -33,8 +34,8 @@
     n_tp, n_cp, nc,
     tok_hbm, rt_hbm, ids_hbm, slot_hbm, wg_hbm, wu_hbm, wd_hbm,
     pr, mix_ref,
-    ids_ref, slot_ref, tok, rt, wg, wu, wd, xs, xr, ps,
-    in_sem, wsem, s1, r1, fs, fr, s2, r2,
+    ids_ref, slot_ref, tok, rt, wg, wu, wd, xs, xr, ps, kept, met,
+    in_sem, wsem, s1, r1, fs, fr, s2, r2, ms,
 ):
     n = n_tp * n_cp
     my_z, my_x = lax.axis_index("tp"), lax.axis_index("cp")
@@ -219,13 +220,37 @@
     mix = mix.T
     mix_hi = mix.astype(jnp.bfloat16)
     mix_lo = (mix - mix_hi.astype(jnp.float32)).astype(jnp.bfloat16)
-    mix_ref[...] = jnp.concatenate([mix_hi, mix_lo], axis=0)
+    mix_ref[...] = jnp.concatenate([mix_hi, mix_lo], axis=1)
 
     for e in range(local):
         for c in range(nc):
             forward(e, c, False)
             if e == 0 or EARLY:
                 forward(e, c, True)
+    rank = jnp.where(half == 0, my_z, my_z - h - 1)
+
+    def merged(z, e):
+        return h < n_tp and MERGE(z, h, e)
+
+    def give_back(e, c, other):
+        pltpu.make_async_remote_copy(
+            src_ref=ps.at[e, c, other],
+            dst_ref=pr.at[e, c, me],
+            send_sem=s2,
+            recv_sem=r2.at[e],
+            device_id=device(jnp.int32(other)),
+            device_id_type=MESH,
+        ).start()
+
+    for z in range(n_tp):
+        for e in range(local):
+            if merged(z, e):
+                @pl.when(my_z == z)
+                def _():
+                    for k in sources(z // h, e, True):
+                        for c in range(nc):
+                            pr[e, c, k] = jnp.zeros(pr.shape[3:], pr.dtype)
+
     for e in range(local):
         gate = jnp.zeros((n * CAP_DEV, ff), jnp.float32)
         up = jnp.zeros((n * CAP_DEV, ff), jnp.float32)
@@ -244,20 +269,51 @@
             cols = pl.ds(c * dc, dc)
             down_copies[e, c].wait()
             part = jnp.dot(hidden, wd[e, :, cols], preferred_element_type=jnp.float32)
-            for i in range(n):
-                ps[e, c, i] = part[i * CAP_DEV:(i + 1) * CAP_DEV].astype(jnp.bfloat16)
             for other in range(n):
-                @pl.when(other != me)
+                z = other // n_cp
+                ps[e, c, other] = part[other * CAP_DEV:(other + 1) * CAP_DEV].astype(jnp.bfloat16)
+                aside = z // h != half
+                direct = other != me
+                if merged(z, e):
+                    direct = direct & jnp.logical_not(aside)
+                @pl.when(direct)
                 def _():
-                    pltpu.make_async_remote_copy(
-                        src_ref=ps.at[e, c, other],
-                        dst_ref=pr.at[e, c, me],
-                        send_sem=s2,
-                        recv_sem=r2,
-                        device_id=device(jnp.int32(other)),
-                        device_id_type=MESH,
-                    ).start()
+                    give_back(e, c, other)
+                if merged(z, e):
+                    at = other % (h * n_cp)
+                    @pl.when(aside & gateway)
+                    def _():
+                        kept[e, c, at] = part[other * CAP_DEV:(other + 1) * CAP_DEV]
+                    for b in pair:
+                        if z // h == b:
+                            continue
+                        @pl.when((half == b) & jnp.logical_not(gateway))
+                        def _():
+                            pltpu.make_async_remote_copy(
+                                src_ref=ps.at[e, c, other],
+                                dst_ref=met.at[e, c, at, rank],
+                                send_sem=s2,
+                                recv_sem=ms.at[e],
+                                device_id={"tp": jnp.int32(inner[b]), "cp": my_x},
+                                device_id_type=MESH,
+                            ).start()
             pr[e, c, me] = ps[e, c, me]
+    for e in range(local):
+        for b in pair if h < n_tp else ():
+            ends = [z * n_cp + x for z in near[1 - b] if merged(z, e) for x in range(n_cp)]
+            if not ends:
+                continue
+            @pl.when(my_z == inner[b])
+            def _():
+                drain(met.at[e, :, pl.ds(0, len(ends))], ms.at[e])
+                for c in range(nc):
+                    for other in ends:
+                        at = other % (h * n_cp)
+                        total = kept[e, c, at]
+                        for m in range(h - 1):
+                            total = total + met[e, c, at, m].astype(jnp.float32)
+                        ps[e, c, other] = total.astype(jnp.bfloat16)
+                        give_back(e, c, other)
     for e in range(local):
         own = h * n_cp - 1
         if h == n_tp or relay[e] == 0:
@@ -272,13 +328,21 @@
         def _():
             drain(xr.at[e, :, pl.ds(0, own + n_cp)], s1.at[e])
     drain(pr.at[:, :, pl.ds(0, n - 1)], s2)
-    drain(pr.at[:, :, pl.ds(0, n - 1)], r2)
+    for e in range(local):
+        counts = [h * n_cp - 1 + n_cp if merged(z, e) else n - 1 for z in range(n_tp)]
+        for count in sorted(set(counts)):
+            here = [z for z in range(n_tp) if counts[z] == count]
+            if len(here) == n_tp:
+                drain(pr.at[e, :, pl.ds(0, count)], r2.at[e])
+                continue
+            @pl.when(functools.reduce(jnp.logical_or, [my_z == z for z in here]))
+            def _():
+                drain(pr.at[e, :, pl.ds(0, count)], r2.at[e])
 
 
 def combine_kernel(pr, mix_ref, out_hbm, ob, osem):
     local, nc, n, cap, dc = pr.shape
     mix = mix_ref[...]
-    half = mix.shape[0] // 2
     part = dc // SPLIT
     outs = []
     for c in range(nc):
@@ -286,8 +350,8 @@
             at = pl.ds(p * part, part)
             cols = pl.ds(c * dc + p * part, part)
             rows = rows_of([pr[e, c, i, :, at] for e in range(local) for i in range(n)])
-            both = jnp.dot(mix, rows, preferred_element_type=jnp.float32)
-            ob[:, cols] = (both[:half] + both[half:]).astype(jnp.bfloat16)
+            rows = jnp.concatenate([rows, rows], axis=0)
+            ob[:, cols] = jnp.dot(mix, rows, preferred_element_type=jnp.float32).astype(jnp.bfloat16)
             copy = pltpu.make_async_copy(ob.at[:, cols], out_hbm.at[:, cols], osem.at[c, p])
             copy.start()
             outs.append(copy)
@@ -306,11 +370,12 @@
     bf16 = jnp.bfloat16
     dma = pltpu.SemaphoreType.DMA
     slab = (local, nc, n, CAP_DEV, dc)
+    across = max(n_tp // 2, 1) * n_cp
     pr, mix = pl.pallas_call(
         functools.partial(exchange_kernel, n_tp, n_cp, nc),
         out_shape=[
             pltpu.VMEM(slab, bf16),
-            pltpu.VMEM((2 * rows, local * n * CAP_DEV), bf16),
+            pltpu.VMEM((rows, 2 * local * n * CAP_DEV), bf16),
         ],
         in_specs=[anywhere] * 7,
         out_specs=[resident, resident],
@@ -325,14 +390,17 @@
             pltpu.VMEM((local, nc, n_cp, CAP_DEV, dc), bf16),
             pltpu.VMEM(slab, bf16),
             pltpu.VMEM(slab, bf16),
+            pltpu.VMEM((local, nc, across, CAP_DEV, dc), jnp.float32),
+            pltpu.VMEM((local, nc, across, max(n_tp // 2 - 1, 1), CAP_DEV, dc), bf16),
             dma((nc + 3,)),
             dma((3, local, nc)),
             dma((local,)),
             dma((local, nc)),
             dma((local, max(n_tp // 2 - 1, 1))),
-            dma((local, nc, max(n_tp // 2, 1) * n_cp)),
+            dma((local, nc, across)),
             dma,
-            dma,
+            dma((local,)),
+            dma((local,)),
         ],
         compiler_params=pltpu.CompilerParams(
             collective_id=0, has_side_effects=True, vmem_limit_bytes=60 * 1024 * 1024

time: 25.1 us -> 24.6 us (0.980)
  Pallas kernels: 25 us -> 24.5 us
    pallas_call x1, Pallas kernels: 23.6 us -> 23.2 us  [body(): pl.pallas_call(functools.partial(exchange_kernel, n_tp, n_cp, nc), out_sh...]
where the time goes in v4:
time: 24.6 us; the launch traced here: 24.5 us
  Pallas kernels  24.5 us (100%)
    pallas_call x1, Pallas kernels, body(): pl.pallas_call(functools.partial(exchange_kernel, n_tp, n_cp, nc), out_sh...  23.2 us
    pallas_call x1, Pallas kernels, body(): pl.pallas_call(combine_kernel, out_shape=jax.ShapeDtypeStruct((rows, widt...  1.24 us

profile of v4, /device:TPU:0, one launch (start us, length us, event | category | flops | bytes accessed | tf_op | source)
XLA Modules:
  0.0 24.5 jit_solution(8198440320573112967)
XLA Ops:
  0.0 23.2 %shard_map.73 = (bf16[2,1,8,2,7168]{4,3,2,1,0:T(2,128)(2,1)S(1)}, bf16[64,64]{1,0:T(8,128)(2,1)S(1)}) custom-call(bf16[64,7168]{1,0:T(8,128)(2,1)} %tok_hbm.1, bf16[4,7168]{1,0:T(4,128)(2,1)} %bitcast.3, s32[2,64]{1,0:T(2,128)} %bitcast.4, s32[2,64]{1,0:T(2,128)} %bitcast.5, bf16[2,7168,256]{2,1,0:T(8,128)(2,1)} %wg_hbm.1, bf16[2,7168,256]{2,1,0:T(8,128)(2,1)} %wu_hbm.1, ...), custom_call_target="tpu_custom_call" | custom-call | tf_op jit(solution)/shard_map/pallas_call | solution.py:374
  23.2 1.2 %shard_map.74 = bf16[64,7168]{1,0:T(8,128)(2,1)} custom-call(bf16[2,1,8,2,7168]{4,3,2,1,0:T(2,128)(2,1)S(1)} %get-tuple-element.7.pr, bf16[64,64]{1,0:T(8,128)(2,1)S(1)} %get-tuple-element.8.mix_ref), custom_call_target="tpu_custom_call" | custom-call | tf_op jit(solution)/shard_map/pallas_call | solution.py:409

commit v5 on v4

--- a/solution.py
+++ b/solution.py
@@ -131,7 +131,7 @@
                     ahead = ahead & gateway
                 @pl.when(ahead)
                 def _():
-                    for x in range(n_cp):
+                    for x in [lax.rem(my_x + i, n_cp) for i in range(1, n_cp + 1)]:
                         place(e, c, z, x, fr.at[e, c, lax.rem(me, h * n_cp)])
 
     def share(e, c):
@@ -190,19 +190,19 @@
                 xs[e, c, x] = outgoing[at:at + CAP_DEV].astype(jnp.bfloat16)
         if c == 0:
             pl.semaphore_wait(barrier, n - 1)
-        cross(0, c)
-        if SHARE_FIRST:
-            share(0, c)
-    if not SHARE_FIRST:
-        for c in range(nc):
-            if local > 1:
-                cross(1, c)
-            share(0, c)
-    for e in range(1, local):
-        for c in range(nc):
-            if SHARE_FIRST or e > 1:
-                cross(e, c)
-            share(e, c)
+        if c == nc - 1:
+            @pl.when(gateway)
+            def _():
+                for e in range(local):
+                    for k in range(nc):
+                        share(e, k)
+                        cross(e, k)
+            @pl.when(jnp.logical_not(gateway))
+            def _():
+                for step in (cross, share):
+                    for e in range(local):
+                        for k in range(nc):
+                            step(e, k)
 
     rt_copy.wait()
     logits = lax.dot_general(rt[...], tok[...], NT, preferred_element_type=jnp.float32)
@@ -269,7 +269,8 @@
             cols = pl.ds(c * dc, dc)
             down_copies[e, c].wait()
             part = jnp.dot(hidden, wd[e, :, cols], preferred_element_type=jnp.float32)
-            for other in range(n):
+            turns = [z * n_cp + x for z in range(n_tp) for x in (reversed(range(n_cp)) if e < local - 1 else range(n_cp))]
+            for other in turns:
                 z = other // n_cp
                 ps[e, c, other] = part[other * CAP_DEV:(other + 1) * CAP_DEV].astype(jnp.bfloat16)
                 aside = z // h != half

time: 24.6 us -> 24.2 us (0.984)
  Pallas kernels: 24.5 us -> 24.1 us
    pallas_call x1, Pallas kernels: 23.2 us -> 22.8 us  [body(): pl.pallas_call(functools.partial(exchange_kernel, n_tp, n_cp, nc), out_sh...]
where the time goes in v5:
time: 24.2 us; the launch traced here: 24.1 us
  Pallas kernels  24.1 us (100%)
    pallas_call x1, Pallas kernels, body(): pl.pallas_call(functools.partial(exchange_kernel, n_tp, n_cp, nc), out_sh...  22.8 us
    pallas_call x1, Pallas kernels, body(): pl.pallas_call(combine_kernel, out_shape=jax.ShapeDtypeStruct((rows, widt...  1.24 us

profile of v5, /device:TPU:0, one launch (start us, length us, event | category | flops | bytes accessed | tf_op | source)
XLA Modules:
  0.0 24.1 jit_solution(17789505511828941401)
XLA Ops:
  0.0 22.8 %shard_map.73 = (bf16[2,1,8,2,7168]{4,3,2,1,0:T(2,128)(2,1)S(1)}, bf16[64,64]{1,0:T(8,128)(2,1)S(1)}) custom-call(bf16[64,7168]{1,0:T(8,128)(2,1)} %tok_hbm.1, bf16[4,7168]{1,0:T(4,128)(2,1)} %bitcast.3, s32[2,64]{1,0:T(2,128)} %bitcast.4, s32[2,64]{1,0:T(2,128)} %bitcast.5, bf16[2,7168,256]{2,1,0:T(8,128)(2,1)} %wg_hbm.1, bf16[2,7168,256]{2,1,0:T(8,128)(2,1)} %wu_hbm.1, ...), custom_call_target="tpu_custom_call" | custom-call | tf_op jit(solution)/shard_map/pallas_call | solution.py:375
  22.9 1.2 %shard_map.74 = bf16[64,7168]{1,0:T(8,128)(2,1)} custom-call(bf16[2,1,8,2,7168]{4,3,2,1,0:T(2,128)(2,1)S(1)} %get-tuple-element.7.pr, bf16[64,64]{1,0:T(8,128)(2,1)S(1)} %get-tuple-element.8.mix_ref), custom_call_target="tpu_custom_call" | custom-call | tf_op jit(solution)/shard_map/pallas_call | solution.py:410

commit v6 on v5

--- a/solution.py
+++ b/solution.py
@@ -33,7 +33,7 @@
 def exchange_kernel(
     n_tp, n_cp, nc,
     tok_hbm, rt_hbm, ids_hbm, slot_hbm, wg_hbm, wu_hbm, wd_hbm,
-    pr, mix_ref,
+    pr, mix_ref, base,
     ids_ref, slot_ref, tok, rt, wg, wu, wd, xs, xr, ps, kept, met,
     in_sem, wsem, s1, r1, fs, fr, s2, r2, ms,
 ):
@@ -339,20 +339,36 @@
             @pl.when(functools.reduce(jnp.logical_or, [my_z == z for z in here]))
             def _():
                 drain(pr.at[e, :, pl.ds(0, count)], r2.at[e])
-
-
-def combine_kernel(pr, mix_ref, out_hbm, ob, osem):
+        if e == local - 2:
+            many = (local - 1) * n * CAP_DEV
+            left = jnp.concatenate([mix_ref[:, :many], mix_ref[:, local * n * CAP_DEV:][:, :many]], axis=1)
+            part = dc // SPLIT
+            for c in range(nc):
+                for p in range(SPLIT):
+                    at = pl.ds(p * part, part)
+                    rows = rows_of([pr[k, c, i, :, at] for k in range(e + 1) for i in range(n)])
+                    rows = jnp.concatenate([rows, rows], axis=0)
+                    base[:, pl.ds(c * dc + p * part, part)] = jnp.dot(
+                        left, rows, preferred_element_type=jnp.float32
+                    )
+    if local == 1:
+        base[...] = jnp.zeros_like(base)
+
+
+def combine_kernel(pr, mix_ref, base, out_hbm, ob, osem):
     local, nc, n, cap, dc = pr.shape
-    mix = mix_ref[...]
+    many, total = (local - 1) * n * cap, local * n * cap
+    mix = jnp.concatenate([mix_ref[:, many:total], mix_ref[:, total + many:]], axis=1)
     part = dc // SPLIT
     outs = []
     for c in range(nc):
         for p in range(SPLIT):
             at = pl.ds(p * part, part)
             cols = pl.ds(c * dc + p * part, part)
-            rows = rows_of([pr[e, c, i, :, at] for e in range(local) for i in range(n)])
+            rows = rows_of([pr[e, c, i, :, at] for e in (local - 1,) for i in range(n)])
             rows = jnp.concatenate([rows, rows], axis=0)
-            ob[:, cols] = jnp.dot(mix, rows, preferred_element_type=jnp.float32).astype(jnp.bfloat16)
+            both = base[:, cols] + jnp.dot(mix, rows, preferred_element_type=jnp.float32)
+            ob[:, cols] = both.astype(jnp.bfloat16)
             copy = pltpu.make_async_copy(ob.at[:, cols], out_hbm.at[:, cols], osem.at[c, p])
             copy.start()
             outs.append(copy)
@@ -372,14 +388,15 @@
     dma = pltpu.SemaphoreType.DMA
     slab = (local, nc, n, CAP_DEV, dc)
     across = max(n_tp // 2, 1) * n_cp
-    pr, mix = pl.pallas_call(
+    pr, mix, base = pl.pallas_call(
         functools.partial(exchange_kernel, n_tp, n_cp, nc),
         out_shape=[
             pltpu.VMEM(slab, bf16),
             pltpu.VMEM((rows, 2 * local * n * CAP_DEV), bf16),
+            pltpu.VMEM((rows, width), jnp.float32),
         ],
         in_specs=[anywhere] * 7,
-        out_specs=[resident, resident],
+        out_specs=[resident, resident, resident],
         scratch_shapes=[
             pltpu.VMEM((expert_ids.shape[1], rows), jnp.int32),
             pltpu.VMEM((slot_index.shape[1], rows), jnp.int32),
@@ -410,14 +427,14 @@
     return pl.pallas_call(
         combine_kernel,
         out_shape=jax.ShapeDtypeStruct((rows, width), bf16),
-        in_specs=[resident, resident],
+        in_specs=[resident, resident, resident],
         out_specs=anywhere,
         scratch_shapes=[
             pltpu.VMEM((rows, width), bf16),
             dma((nc, SPLIT)),
         ],
         compiler_params=pltpu.CompilerParams(vmem_limit_bytes=8 * 1024 * 1024),
-    )(pr, mix)
+    )(pr, mix, base)
 
 
 def solution(mesh):

time: 24.2 us -> 24.2 us (level)
  no operation moved by 1% of the time
where the time goes in v6:
time: 24.2 us; the launch traced here: 24.1 us
  Pallas kernels  24.1 us (100%)
    pallas_call x1, Pallas kernels, body(): pl.pallas_call(functools.partial(exchange_kernel, n_tp, n_cp, nc), out_sh...  22.8 us
    pallas_call x1, Pallas kernels, body(): pl.pallas_call(combine_kernel, out_shape=jax.ShapeDtypeStruct((rows, widt...  1.24 us

profile of v6, /device:TPU:0, one launch (start us, length us, event | category | flops | bytes accessed | tf_op | source)
XLA Modules:
  0.0 24.1 jit_solution(18282726910317195156)
XLA Ops:
  0.0 22.8 %shard_map.73 = (bf16[2,1,8,2,7168]{4,3,2,1,0:T(2,128)(2,1)S(1)}, bf16[64,64]{1,0:T(8,128)(2,1)S(1)}, f32[64,7168]{1,0:T(8,128)S(1)}) custom-call(bf16[64,7168]{1,0:T(8,128)(2,1)} %tok_hbm.1, bf16[4,7168]{1,0:T(4,128)(2,1)} %bitcast.3, s32[2,64]{1,0:T(2,128)} %bitcast.4, s32[2,64]{1,0:T(2,128)} %bitcast.5, bf16[2,7168,256]{2,1,0:T(8,128)(2,1)} %wg_hbm.1, ...), custom_call_target="tpu_custom_call" | custom-call | tf_op jit(solution)/shard_map/pallas_call | solution.py:391
  22.9 1.2 %shard_map.74 = bf16[64,7168]{1,0:T(8,128)(2,1)} custom-call(bf16[2,1,8,2,7168]{4,3,2,1,0:T(2,128)(2,1)S(1)} %get-tuple-element.8.pr, bf16[64,64]{1,0:T(8,128)(2,1)S(1)} %get-tuple-element.9.mix_ref, f32[64,7168]{1,0:T(8,128)S(1)} %get-tuple-element.10.base), custom_call_target="tpu_custom_call" | custom-call | tf_op jit(solution)/shard_map/pallas_call | solution.py:427
